TPU v7x, 256 devices: a whole 4x4x8 slice. The times are simulated.
256 devices in a mesh: samp: 4 (over y), var: 64 (over x, z, core).
Axes of the slice: x: 4, y: 4, z: 8, core: 2. Of those that a mesh axis runs over, the one named last changes fastest.
Arguments:
- samples: bfloat16 [1024, 262144], P('samp', 'var'), may hold values from -6 to 6
- precision_blocks: bfloat16 [1024, 3, 256, 256], P('var'), may hold values from -6 to 6
- pair_rows: int32 [1024, 3], P('var'), may hold values from 0 to 1023, as said below
Outputs:
- gradient: float32 [1024, 3, 256, 256], P('var', None, 'samp')
Inputs may be any that keep to these rules, and one draw needn't show every extreme that they name: pair_rows[j, 0] = j. For k >= 1, pair_rows[j, k] = j XOR (16 * c) with c a nonzero value below the number of indices of var that depends only on k and j mod 16, so pair_rows[pair_rows[j, k], k] = j. Over the off-diagonal slots of the blocks of one index of var, at most 1 partners lie on any one other index, and some pair of indices reaches 1.
All inputs are finite; a program needn't handle non-finite values.
Results may differ from a plain program's by a relative error of at most 0.0019.
Values may be sent and summed in bfloat16 or wider, within the bound.
A program may use at most 128 MiB of HBM per device.

v0:
```python
import jax
import jax.numpy as jnp
from jax import lax
from jax.sharding import PartitionSpec as P


def slot_ranks(peer_index, order_keys):
    same_peer = peer_index[:, None] == peer_index[None, :]
    before = order_keys[None, :] < order_keys[:, None]
    return jnp.sum(jnp.where(same_peer & before, 1, 0), axis=1).astype(jnp.int32)


def shards(samples, precision_blocks, pair_rows):
    var_count = lax.axis_size("var")
    samp_count = lax.axis_size("samp")
    local_rows = samples.shape[0]
    per_dev, slot_count, block_width, _ = precision_blocks.shape
    levels = slot_count - 1
    entries = levels * per_dev
    capacity = (entries + var_count - 2) // (var_count - 1)
    norm_factor = 0.5 / (local_rows * samp_count)
    blocks = samples.reshape(local_rows, per_dev, block_width)
    partners = pair_rows[:, 1:].T.reshape(entries)
    peer_index = partners // per_dev
    partner_local = partners % per_dev
    level_index = jnp.repeat(jnp.arange(levels, dtype=jnp.int32), per_dev)
    own_local = jnp.tile(jnp.arange(per_dev, dtype=jnp.int32), levels)
    send_slot = peer_index * capacity + slot_ranks(peer_index, level_index * per_dev + own_local)
    recv_slot = peer_index * capacity + slot_ranks(
        peer_index, level_index * per_dev + partner_local
    )
    outgoing = jnp.zeros((local_rows, var_count * capacity, block_width), jnp.bfloat16)
    outgoing = outgoing.at[:, send_slot, :].set(blocks[:, own_local, :])
    incoming = lax.all_to_all(outgoing, "var", split_axis=1, concat_axis=1, tiled=True)
    fetched = incoming[:, recv_slot, :].reshape(local_rows, levels, per_dev, block_width)
    mixed_cols = jnp.einsum(
        "ntb,tbc->ntc", blocks, precision_blocks[:, 0], preferred_element_type=jnp.float32
    )
    mixed_cols = mixed_cols + jnp.einsum(
        "nktb,tkbc->ntc", fetched, precision_blocks[:, 1:], preferred_element_type=jnp.float32
    )
    mixed_cols = mixed_cols.astype(jnp.bfloat16)
    own_diag = jnp.einsum("ntb,ntc->tbc", blocks, mixed_cols, preferred_element_type=jnp.float32)
    own_off = jnp.einsum("nktb,ntc->tkbc", fetched, mixed_cols, preferred_element_type=jnp.float32)
    outgoing_mixed = jnp.zeros((local_rows, var_count * capacity, block_width), jnp.bfloat16)
    outgoing_mixed = outgoing_mixed.at[:, send_slot, :].set(mixed_cols[:, own_local, :])
    incoming_mixed = lax.all_to_all(outgoing_mixed, "var", split_axis=1, concat_axis=1, tiled=True)
    fetched_mixed = incoming_mixed[:, recv_slot, :].reshape(
        local_rows, levels, per_dev, block_width
    )
    other_diag = jnp.einsum("nts,ntc->tsc", mixed_cols, blocks, preferred_element_type=jnp.float32)
    other_off = jnp.einsum(
        "nkts,ntc->tksc", fetched_mixed, blocks, preferred_element_type=jnp.float32
    )
    summed = jnp.concatenate([(own_diag + other_diag)[:, None], own_off + other_off], axis=1)
    reduced = lax.psum_scatter(summed, "samp", scatter_dimension=2, tiled=True)
    return reduced * norm_factor


def solution(mesh):
    placed = (P("samp", "var"), P("var", None, None, None), P("var", None))
    return jax.shard_map(
        shards, mesh=mesh, in_specs=placed, out_specs=P("var", None, "samp", None), check_vma=False
    )
```

profile of v0, /device:TPU:1, one launch (start us, length us, event | category | flops | bytes accessed | tf_op | source)
XLA Modules:
  0.0 620.6 jit_solution(6293909588162080464)
XLA Ops:
  6.5 0.7 slice_bitcast_fusion
  7.2 0.1 reshape.269
  7.3 0.1 reshape.268
  7.4 0.1 mul.32
  7.5 0.1 tile.20
  7.6 0.1 tile.18
  7.7 3.3 copy.40
  10.9 2.4 copy.42
  13.3 0.2 select_reduce_fusion
  13.5 4.3 gather_fusion
  17.9 4.2 broadcast.235.clone
  22.1 11.4 %scatter_fusion = bf16[256,64,256]{2,0,1:T(8,128)(2,1)} fusion(bf16[256,64,256]{2,0,1:T(8,128)(2,1)} %broadcast.235.clone, s32[32]{0:T(128)S(1)} %fusion.18, bf16[32,256,256]{2,1,0:T(8,128)(2,1)} %gather_fusion), kind=kCustom, calls=%fused_computation.4 | custom fusion | bytes 12583040 | tf_op jit(solution)/shard_map/scatter | solution.py:33
  33.5 13.2 %all-to-all-start = ((bf16[256,64,256]{2,0,1:T(8,128)(2,1)}), bf16[256,64,256]{2,0,1:T(8,128)(2,1)}, u32[]{:S(2)}, u32[]{:S(2)}) async-start(bf16[256,64,256]{2,0,1:T(8,128)(2,1)} %scatter_fusion), calls=%async_computation | async-start | bytes 16777216 | tf_op jit(solution)/shard_map/all_to_all | solution.py:34
  46.7 4.3 fusion.13
  51.0 181.4 %all-to-all-done = bf16[256,64,256]{2,0,1:T(8,128)(2,1)} async-done(((bf16[256,64,256]{2,0,1:T(8,128)(2,1)}), bf16[256,64,256]{2,0,1:T(8,128)(2,1)}, u32[]{:S(2)}, u32[]{:S(2)}) %all-to-all-start) | async-done | bytes 8388640 | tf_op jit(solution)/shard_map/all_to_all | solution.py:34
  232.4 6.2 gather_fusion.1
  238.6 7.3 %fusion.2 = bf16[256,16,256]{0,2,1:T(8,128)(2,1)} fusion(f32[16,256,256]{2,1,0:T(8,128)} %fusion.13, bf16[256,2,16,256]{3,0,2,1:T(8,128)(2,1)} %bitcast.63, bf16[16,3,256,256]{3,2,1,0:T(8,128)(2,1)} %param.4), kind=kOutput, calls=%fused_computation.10 | convolution fusion | flops 1075838976 | bytes 14680064 | tf_op jit(solution)/shard_map/nktb,tkbc->ntc/dot_general | solution.py:39
  245.9 4.3 gather_fusion.2
  250.3 6.4 %copy.49 = bf16[32,256,256]{2,1,0:T(8,128)(2,1)} copy(bf16[32,256,256]{1,2,0:T(8,128)(2,1)} %gather_fusion.2) | data formatting | bytes 8388608 | tf_op jit(solution)/shard_map/gather | solution.py:46
  256.7 4.2 broadcast.235
  260.9 11.4 %scatter_fusion.1 = bf16[256,64,256]{2,0,1:T(8,128)(2,1)} fusion(bf16[256,64,256]{2,0,1:T(8,128)(2,1)} %broadcast.235, s32[32]{0:T(128)S(1)} %fusion.18, bf16[32,256,256]{2,1,0:T(8,128)(2,1)} %copy.49), kind=kCustom, calls=%fused_computation.5 | custom fusion | bytes 12583040 | tf_op jit(solution)/shard_map/scatter | solution.py:46
  272.3 6.1 all-to-all-start.1
  278.4 0.2 reduce-scatter.2.cloned.1.call-start
  278.6 4.3 fusion.22
  282.9 5.4 copy.46
  288.3 6.1 fusion.7
  294.3 169.8 %all-to-all-done.1 = bf16[256,64,256]{2,0,1:T(8,128)(2,1)} async-done(((bf16[256,64,256]{2,0,1:T(8,128)(2,1)}), bf16[256,64,256]{2,0,1:T(8,128)(2,1)}, u32[]{:S(2)}, u32[]{:S(2)}) %all-to-all-start.1) | async-done | bytes 8388640 | tf_op jit(solution)/shard_map/all_to_all | solution.py:47
  464.1 6.2 gather_fusion.3
  470.3 0.0 copy-start
  470.3 0.0 copy-start.1
  470.3 6.9 %fusion.3 = f32[16,2,256,256]{3,2,1,0:T(8,128)} fusion(bf16[256,16,256,1]{0,2,3,1:T(8,128)(2,1)S(1)} %bitcast.62, bf16[256,2,16,256]{3,0,2,1:T(8,128)(2,1)} %bitcast.65), kind=kOutput, calls=%fused_computation.11 | convolution fusion | flops 1073741824 | bytes 14680064 | tf_op jit(solution)/shard_map/nkts,ntc->tksc/dot_general | solution.py:52
  477.2 0.0 copy-done
  477.2 0.0 copy-done.1
  477.2 8.2 %fusion.8 = f32[16,2,256,256]{3,2,1,0:T(8,128)} fusion(f32[16,2,256,256]{3,2,1,0:T(8,128)} %fusion.3, bf16[256,2,16,256]{3,0,2,1:T(8,128)(2,1)S(1)} %bitcast.64, bf16[256,16,256]{0,2,1:T(8,128)(2,1)S(1)} %copy-done), kind=kOutput, calls=%fused_computation.17 | convolution fusion | flops 1075838976 | bytes 23068672 | tf_op jit(solution)/shard_map/nktb,ntc->tkbc/dot_general | solution.py:44
  485.4 10.6 %pad_maximum_fusion = f32[16,3,256,256]{3,2,1,0:T(8,128)} fusion(f32[16,2,256,256]{3,2,1,0:T(8,128)} %fusion.8, f32[16,1,256,256]{3,2,1,0:T(8,128)} %fusion.7), kind=kLoop, calls=%fused_computation.6 | loop fusion | flops 3145728 | bytes 25165824 | tf_op jit(solution)/shard_map/concatenate | solution.py:55
  495.9 0.0 reduce-scatter.2.cloned.1.call-update
  496.0 113.8 %reduce-scatter.2.cloned.1.call-done = f32[16,3,64,256]{3,2,1,0:T(8,128)} async-done(((f32[16,3,256,256]{3,2,1,0:T(8,128)}), f32[16,3,64,256]{3,2,1,0:T(8,128)}) %reduce-scatter.2.cloned.1.call-update) | async-done | bytes 3145744 | tf_op jit(solution)/shard_map/reduce_scatter | solution.py:56
  609.8 3.9 broadcast_multiply_fusion
  (9 shorter events, 0.1 us)
Async XLA Ops:
  33.5 198.9 %all-to-all-start = ((bf16[256,64,256]{2,0,1:T(8,128)(2,1)}), bf16[256,64,256]{2,0,1:T(8,128)(2,1)}, u32[]{:S(2)}, u32[]{:S(2)}) async-start(bf16[256,64,256]{2,0,1:T(8,128)(2,1)} %scatter_fusion), calls=%async_computation | async-start | bytes 16777216 | tf_op jit(solution)/shard_map/all_to_all | solution.py:34
  272.3 191.8 %all-to-all-start.1 = ((bf16[256,64,256]{2,0,1:T(8,128)(2,1)}), bf16[256,64,256]{2,0,1:T(8,128)(2,1)}, u32[]{:S(2)}, u32[]{:S(2)}) async-start(bf16[256,64,256]{2,0,1:T(8,128)(2,1)} %scatter_fusion.1), calls=%async_computation.1 | async-start | bytes 16777216 | tf_op jit(solution)/shard_map/all_to_all | solution.py:47
  278.4 331.4 %reduce-scatter.2.cloned.1.call-start = ((), (), s32[]{:S(2)}) async-start(), calls=%async_computation.3 | async-start | bytes 15728640 | tf_op jit(solution)/shard_map/reduce_scatter | solution.py:56
  470.3 6.9 %copy-start = (bf16[256,16,256]{0,2,1:T(8,128)(2,1)S(1)}, bf16[256,16,256]{0,2,1:T(8,128)(2,1)}, u32[]{:S(2)}) copy-start(bf16[256,16,256]{0,2,1:T(8,128)(2,1)} %fusion.2) | copy-start | bytes 6291460
  470.3 6.9 %copy-start.1 = (bf16[32,256,256]{2,1,0:T(8,128)(2,1)S(1)}, bf16[32,256,256]{2,1,0:T(8,128)(2,1)}, u32[]{:S(2)}) copy-start(bf16[32,256,256]{2,1,0:T(8,128)(2,1)} %gather_fusion.1) | copy-start | bytes 12582916
Sparse Core Ops, SparseCore 0:
  496.1 113.6 reduce-scatter.1
where the time goes:
time: 621 us
  waiting for transfers between devices  465 us (75%)
  local copies, waits for them, and re-layouts  70.7 us (11%)
  matrix products  31.1 us (5%)
  other arithmetic  20.8 us (3%)
  starting transfers between devices  19.5 us (3%)
  between operations  13.5 us (2%)
    all_to_all x1, waiting for transfers between devices, shards(): lax.all_to_all(outgoing, 'var', split_axis=1, concat_axis=1, tiled=True)  181 us
    all_to_all x1, waiting for transfers between devices, shards(): lax.all_to_all(outgoing_mixed, 'var', split_axis=1, concat_axis=1, tiled=...  170 us
    reduce_scatter x1, waiting for transfers between devices, shards(): reduced = lax.psum_scatter(summed, 'samp', scatter_dimension=2, tiled=True)  114 us
    all_to_all x1, starting transfers between devices, shards(): lax.all_to_all(outgoing, 'var', split_axis=1, concat_axis=1, tiled=True)  13.2 us
  transfers between devices with their start and end apart: 3, of which 3 were waited for; matrix products, arithmetic and copies ran while one was open for 3% of the time, Pallas kernels for 0%

commit v1 on v0

v1 whole, which is shorter than its diff:
```python
import jax
import jax.numpy as jnp
from jax import lax
from jax.experimental import pallas as pl
from jax.experimental.pallas import tpu as pltpu
from jax.sharding import PartitionSpec as P


def pick_columns(columns, samples, width, group):
    rows, total = samples.shape
    count = columns.shape[0]
    group = min(group, count)

    def body(index_ref, x_ref, o_ref):
        first = pl.program_id(0) * group
        for i in range(group):
            start = pl.multiple_of(index_ref[first + i] * width, width)
            o_ref[i] = x_ref[:, pl.ds(start, width)]

    return pl.pallas_call(
        body,
        out_shape=jax.ShapeDtypeStruct((count, rows, width), samples.dtype),
        grid_spec=pltpu.PrefetchScalarGridSpec(
            num_scalar_prefetch=1,
            grid=(count // group,),
            in_specs=[pl.BlockSpec((rows, total), lambda g, index: (0, 0))],
            out_specs=pl.BlockSpec((group, rows, width), lambda g, index: (g, 0, 0)),
        ),
        name="pick_columns",
    )(columns, samples)


def pick_blocks(picked, blocks, group):
    _, rows, width = blocks.shape
    count = picked.shape[0]
    group = min(group, count)

    def body(index_ref, *refs):
        for i in range(group):
            refs[group][i] = refs[i][0]

    def source(i):
        return pl.BlockSpec((1, rows, width), lambda g, index: (index[g * group + i], 0, 0))

    return pl.pallas_call(
        body,
        out_shape=jax.ShapeDtypeStruct((count, rows, width), blocks.dtype),
        grid_spec=pltpu.PrefetchScalarGridSpec(
            num_scalar_prefetch=1,
            grid=(count // group,),
            in_specs=[source(i) for i in range(group)],
            out_specs=pl.BlockSpec((group, rows, width), lambda g, index: (g, 0, 0)),
        ),
        name="pick_blocks",
    )(picked, *([blocks] * group))


def gradient_terms(group_index, own, fetched, precision, norm_factor):
    chunks, per_group, rows, width = own.shape
    levels = fetched.shape[1]
    slots = levels + 1
    part = width // chunks

    def body(index_ref, own_ref, fetched_ref, p_ref, rows_ref, turned_ref):
        totals = [jnp.zeros((width, width), jnp.float32) for _ in range(slots)]
        for s in range(chunks):
            factors = [own_ref[s, 0]] + [fetched_ref[s, k, 0] for k in range(levels)]
            mixed = jnp.zeros((rows, width), jnp.float32)
            for k in range(slots):
                mixed = mixed + jnp.dot(factors[k], p_ref[0, k], preferred_element_type=jnp.float32)
            mixed = mixed.astype(jnp.bfloat16)
            for k in range(slots):
                totals[k] = totals[k] + lax.dot_general(
                    factors[k], mixed, (((0,), (0,)), ((), ())), preferred_element_type=jnp.float32
                )
        for k in range(slots):
            scaled = totals[k] * norm_factor
            turned = scaled.T
            if k == 0:
                scaled = scaled + turned
            for s in range(chunks):
                rows_ref[s, 0, k] = scaled[s * part : (s + 1) * part]
                if k > 0:
                    turned_ref[s, 0, k - 1] = turned[s * part : (s + 1) * part].astype(jnp.bfloat16)

    return pl.pallas_call(
        body,
        out_shape=(
            jax.ShapeDtypeStruct((chunks, per_group, slots, part, width), jnp.float32),
            jax.ShapeDtypeStruct((chunks, per_group, levels, part, width), jnp.bfloat16),
        ),
        grid_spec=pltpu.PrefetchScalarGridSpec(
            num_scalar_prefetch=1,
            grid=(per_group,),
            in_specs=[
                pl.BlockSpec((chunks, 1, rows, width), lambda t, g: (0, t, 0, 0)),
                pl.BlockSpec((chunks, levels, 1, rows, width), lambda t, g: (0, 0, t, 0, 0)),
                pl.BlockSpec((1, slots, width, width), lambda t, g: (g[0] * per_group + t, 0, 0, 0)),
            ],
            out_specs=[
                pl.BlockSpec((chunks, 1, slots, part, width), lambda t, g: (0, t, 0, 0, 0)),
                pl.BlockSpec((chunks, 1, levels, part, width), lambda t, g: (0, t, 0, 0, 0)),
            ],
        ),
        name="gradient_terms",
    )(group_index, own, fetched, precision)


def add_turned(slots_of, own_rows, incoming):
    count, slots, part, width = own_rows.shape
    levels = slots - 1

    def body(index_ref, rows_ref, *refs):
        out_ref = refs[levels]
        out_ref[0, 0] = rows_ref[0, 0]
        for k in range(levels):
            out_ref[0, k + 1] = rows_ref[0, k + 1] + refs[k][0].astype(jnp.float32)

    def source(k):
        return pl.BlockSpec((1, part, width), lambda t, index: (index[t * levels + k], 0, 0))

    return pl.pallas_call(
        body,
        out_shape=jax.ShapeDtypeStruct(own_rows.shape, jnp.float32),
        grid_spec=pltpu.PrefetchScalarGridSpec(
            num_scalar_prefetch=1,
            grid=(count,),
            in_specs=[pl.BlockSpec((1, slots, part, width), lambda t, index: (t, 0, 0, 0))]
            + [source(k) for k in range(levels)],
            out_specs=pl.BlockSpec((1, slots, part, width), lambda t, index: (t, 0, 0, 0)),
        ),
        name="add_turned",
    )(slots_of, own_rows, *([incoming] * levels))


def shards(samples, precision_blocks, pair_rows):
    peers = lax.axis_size("var")
    chunks = lax.axis_size("samp")
    rows = samples.shape[0]
    count, slots, width, _ = precision_blocks.shape
    levels = slots - 1
    per_group = count // chunks
    entries = levels * count
    part = width // chunks
    norm_factor = 0.5 / (rows * chunks)

    partners = pair_rows[:, 1:] // count
    owner = partners.reshape(entries)
    entry_ids = lax.iota(jnp.int32, entries)
    hit = owner[None, :] == lax.iota(jnp.int32, peers)[:, None]
    entry_to = jnp.sum(jnp.where(hit, entry_ids[None, :], 0), axis=1).astype(jnp.int32)

    everything = lax.iota(jnp.int32, count)
    own = pick_columns(everything, samples, width, 4)
    own = lax.all_to_all(own, "samp", 0, 0, tiled=True)
    own = own.reshape(chunks, per_group, rows, width)

    outgoing = pick_columns(entry_to // levels, samples, width, 8)
    incoming = lax.all_to_all(outgoing, "var", 0, 0, tiled=True)
    by_group = jnp.transpose(partners.reshape(chunks, per_group, levels), (0, 2, 1)).reshape(entries)
    fetched = pick_blocks(by_group, incoming, 4)
    fetched = lax.all_to_all(fetched, "samp", 0, 0, tiled=True)
    fetched = fetched.reshape(chunks, levels, per_group, rows, width)

    group_index = lax.axis_index("samp").astype(jnp.int32).reshape(1)
    own_rows, turned = gradient_terms(group_index, own, fetched, precision_blocks, norm_factor)

    turned = lax.all_to_all(turned.reshape(chunks * per_group * levels, part, width), "samp", 0, 0, tiled=True)
    own_rows = lax.all_to_all(own_rows.reshape(count, slots, part, width), "samp", 0, 0, tiled=True)
    sent = pick_blocks(entry_to, turned, 8)
    received = lax.all_to_all(sent, "var", 0, 0, tiled=True)
    return add_turned(owner, own_rows, received)


def solution(mesh):
    placed = (P("samp", "var"), P("var", None, None, None), P("var", None))
    return jax.shard_map(
        shards, mesh=mesh, in_specs=placed, out_specs=P("var", None, "samp", None), check_vma=False
    )
```

time: 621 us -> 433 us (0.70)
  waiting for transfers between devices: 465 us -> 277 us
  blocking collectives: 0 us -> 79.4 us
  local copies, waits for them, and re-layouts: 70.7 us -> 2.75 us
  Pallas kernels: 0 us -> 45.5 us
  matrix products: 31.1 us -> 0 us
  other arithmetic: 20.8 us -> 1.3 us
  between operations: 13.5 us -> 0.05 us
  starting transfers between devices: 19.5 us -> 25.9 us
    reduce_scatter x1 -> x0, waiting for transfers between devices: 114 us -> none  [shards(): reduced = lax.psum_scatter(summed, 'samp', scatter_dimension=2, tiled=True)]
    all_to_all x0 -> x2, blocking collectives: none -> 79.4 us  [the longest x1 61.7 us: shards(): received = lax.all_to_all(sent, 'var', 0, 0, tiled=True)]
    all_to_all x2 -> x4, waiting for transfers between devices: 351 us -> 277 us  [the longest x1 181 us: shards(): incoming = lax.all_to_all(outgoing, 'var', 0, 0, tiled=True)]
    pallas_call x0 -> x6, Pallas kernels: none -> 45.5 us  [the longest x2 13.6 us: pick_blocks(): pl.pallas_call(body, out_shape=jax.ShapeDtypeStruct((count, rows, width),...]
    dot_general x5 -> x0, matrix products: 31.1 us -> none  [the longest x1 8.21 us: shards(): jnp.einsum('nktb,ntc->tkbc', fetched, mixed_cols, preferred_element_type=...]
    gather x5 -> x0, local copies, waits for them, and re-layouts: 27.4 us -> none  [the longest x2 10.7 us: shards(): mixed_cols[:, own_local, :]]
    scatter x2 -> x0, local copies, waits for them, and re-layouts: 22.7 us -> none  [the longest x1 11.4 us: shards(): outgoing = outgoing.at[:, send_slot, :].set(blocks[:, own_local, :])]
    concatenate x1 -> x0, other arithmetic: 10.6 us -> none  [shards(): jnp.concatenate([(own_diag + other_diag)[:, None], own_off + other_off],...]
  transfers between devices with their start and end apart: 3 -> 4, of which waited for: 3 -> 4; matrix products, arithmetic and copies ran while one was open for 3% -> 0% of each run, Pallas kernels for 0% -> 4%
where the time goes in v1:
time: 433 us; the launch traced here: 431 us
  waiting for transfers between devices  277 us (64%)
  blocking collectives  79.4 us (18%)
  Pallas kernels  45.5 us (11%)
  starting transfers between devices  25.9 us (6%)
    all_to_all x1, waiting for transfers between devices, shards(): incoming = lax.all_to_all(outgoing, 'var', 0, 0, tiled=True)  181 us
    all_to_all x1, blocking collectives, shards(): received = lax.all_to_all(sent, 'var', 0, 0, tiled=True)  61.7 us
    all_to_all x1, waiting for transfers between devices, shards(): fetched = lax.all_to_all(fetched, 'samp', 0, 0, tiled=True)  48.2 us
    all_to_all x1, waiting for transfers between devices, shards(): lax.all_to_all(own_rows.reshape(count, slots, part, width), 'samp', 0, 0,...  28.7 us
    all_to_all x1, waiting for transfers between devices, shards(): own = lax.all_to_all(own, 'samp', 0, 0, tiled=True)  18.6 us
    all_to_all x1, blocking collectives, shards(): lax.all_to_all(turned.reshape(chunks * per_group * levels, part, width),...  17.8 us
    pallas_call x2, Pallas kernels, pick_blocks(): pl.pallas_call(body, out_shape=jax.ShapeDtypeStruct((count, rows, width),...  13.6 us
    all_to_all x1, starting transfers between devices, shards(): incoming = lax.all_to_all(outgoing, 'var', 0, 0, tiled=True)  13.2 us
  transfers between devices with their start and end apart: 4, of which 4 were waited for; matrix products, arithmetic and copies ran while one was open for 0% of the time, Pallas kernels for 4%

profile of v1, /device:TPU:1, one launch (start us, length us, event | category | flops | bytes accessed | tf_op | source)
XLA Modules:
  0.0 431.4 jit_solution(5647150201984618090)
XLA Ops:
  0.0 0.7 and_select_fusion.1
  0.7 0.1 copy.8
  0.8 0.1 reshape.25.index_ref
  0.9 0.0 copy-start.2
  0.9 0.1 select_reduce_fusion.index_ref
  1.0 0.0 copy-start.3
  1.0 0.5 and_select_fusion.index_ref
  1.5 7.3 %pick_columns.3 = bf16[64,256,256]{2,1,0:T(8,128)(2,1)} custom-call(s32[64]{0:T(128)} %and_select_fusion.index_ref, bf16[256,4096]{1,0:T(8,128)(2,1)} %x_ref.3), custom_call_target="tpu_custom_call" | custom-call | tf_op jit(solution)/shard_map/pick_columns/pallas_call | solution.py:20
  8.7 0.0 copy-done.2
  8.8 0.0 copy-done.3
  8.8 13.2 %all-to-all-start.1 = ((bf16[64,256,256]{2,1,0:T(8,128)(2,1)}), bf16[64,256,256]{2,1,0:T(8,128)(2,1)}, u32[]{:S(2)}, u32[]{:S(2)}) async-start(bf16[64,256,256]{2,1,0:T(8,128)(2,1)} %pick_columns.3), calls=%async_computation.1 | async-start | bytes 16777216 | tf_op jit(solution)/shard_map/all_to_all | solution.py:159
  21.9 0.6 iota.11.index_ref
  22.5 4.2 pick_columns.2
  26.7 181.0 %all-to-all-done.1.refs_0_.refs_1_.refs_2_.refs_3_ = bf16[64,256,256]{2,1,0:T(8,128)(2,1)} async-done(((bf16[64,256,256]{2,1,0:T(8,128)(2,1)}), bf16[64,256,256]{2,1,0:T(8,128)(2,1)}, u32[]{:S(2)}, u32[]{:S(2)}) %all-to-all-start.1) | async-done | bytes 8388640 | tf_op jit(solution)/shard_map/all_to_all | solution.py:159
  207.7 4.2 all-to-all-start
  211.8 0.1 reshape.28
  211.9 0.6 reshape.29.index_ref
  212.5 7.3 %pick_blocks.2 = bf16[32,256,256]{2,1,0:T(8,128)(2,1)} custom-call(s32[32]{0:T(128)} %reshape.29.index_ref, bf16[64,256,256]{2,1,0:T(8,128)(2,1)} %all-to-all-done.1.refs_0_.refs_1_.refs_2_.refs_3_, bf16[64,256,256]{2,1,0:T(8,128)(2,1)} %all-to-all-done.1.refs_0_.refs_1_.refs_2_.refs_3_, ...), custom_call_target="tpu_custom_call" | custom-call | tf_op jit(solution)/shard_map/pick_blocks/pallas_call | solution.py:45
  219.8 18.6 %all-to-all-done = bf16[16,256,256]{2,1,0:T(8,128)(2,1)S(1)} async-done(((bf16[16,256,256]{2,1,0:T(8,128)(2,1)}), bf16[16,256,256]{2,1,0:T(8,128)(2,1)S(1)}, u32[]{:S(2)}, u32[]{:S(2)}) %all-to-all-start) | async-done | bytes 2097184 | tf_op jit(solution)/shard_map/all_to_all | solution.py:155
  238.4 0.0 copy-start.1
  238.4 1.3 copy-done.1
  239.7 4.8 %all-to-all-start.2 = ((bf16[32,256,256]{2,1,0:T(8,128)(2,1)}), bf16[32,256,256]{2,1,0:T(8,128)(2,1)}, u32[]{:S(2)}, u32[]{:S(2)}) async-start(bf16[32,256,256]{2,1,0:T(8,128)(2,1)} %pick_blocks.2), calls=%async_computation.2 | async-start | bytes 8388608 | tf_op jit(solution)/shard_map/all_to_all | solution.py:162
  244.6 48.2 %all-to-all-done.2 = bf16[32,256,256]{2,1,0:T(8,128)(2,1)} async-done(((bf16[32,256,256]{2,1,0:T(8,128)(2,1)}), bf16[32,256,256]{2,1,0:T(8,128)(2,1)}, u32[]{:S(2)}, u32[]{:S(2)}) %all-to-all-start.2) | async-done | bytes 4194336 | tf_op jit(solution)/shard_map/all_to_all | solution.py:162
  292.8 9.7 %gradient_terms.1 = (f32[4,4,3,64,256]{4,3,2,1,0:T(8,128)}, bf16[4,4,2,64,256]{4,3,2,1,0:T(8,128)(2,1)}) custom-call(s32[1]{0:T(128)} %bitcast.index_ref, bf16[4,4,256,256]{3,2,1,0:T(8,128)(2,1)} %bitcast.8, bf16[4,2,4,256,256]{4,3,2,1,0:T(8,128)(2,1)} %bitcast.3.fetched_ref, bf16[16,3,256,256]{3,2,1,0:T(8,128)(2,1)} %p_ref.1), custom_call_target="tpu_custom_call" | custom-call | tf_op jit(solution)/shard_map/gradient_terms/pallas_call | solution.py:86
  302.6 17.8 %all_to_all.30.refs_0_.refs_1_.refs_2_.refs_3_.refs_4_.refs_5_.refs_6_.refs_7_ = bf16[32,64,256]{2,1,0:T(8,128)(2,1)} all-to-all(bf16[32,64,256]{2,1,0:T(8,128)(2,1)} %bitcast.10), channel_id=1, replica_groups=mesh['samp'=4,'var'=64] {'samp'}, dimensions={0} | all-to-all | bytes 2097152 | tf_op jit(solution)/shard_map/all_to_all | solution.py:168
  320.3 3.7 all-to-all-start.3
  324.1 6.3 %pick_blocks.3 = bf16[64,64,256]{2,1,0:T(8,128)(2,1)} custom-call(s32[64]{0:T(128)} %copy-done.3, bf16[32,64,256]{2,1,0:T(8,128)(2,1)} %all_to_all.30.refs_0_.refs_1_.refs_2_.refs_3_.refs_4_.refs_5_.refs_6_.refs_7_, bf16[32,64,256]{2,1,0:T(8,128)(2,1)} %all_to_all.30.refs_0_.refs_1_.refs_2_.refs_3_.refs_4_.refs_5_.refs_6_.refs_7_, ...), custom_call_target="tpu_custom_call" | custom-call | tf_op jit(solution)/shard_map/pick_blocks/pallas_call | solution.py:45
  330.4 28.7 %all-to-all-done.3.rows_ref = f32[16,3,64,256]{3,2,1,0:T(8,128)S(1)} async-done(((f32[16,3,64,256]{3,2,1,0:T(8,128)}), f32[16,3,64,256]{3,2,1,0:T(8,128)S(1)}, u32[]{:S(2)}, u32[]{:S(2)}) %all-to-all-start.3) | async-done | bytes 3145760 | tf_op jit(solution)/shard_map/all_to_all | solution.py:169
  359.1 0.0 copy-start
  359.1 61.7 %all_to_all.31.refs_0_.refs_1_ = bf16[64,64,256]{2,1,0:T(8,128)(2,1)} all-to-all(bf16[64,64,256]{2,1,0:T(8,128)(2,1)} %pick_blocks.3), channel_id=1, replica_groups=mesh['samp'=4,'var'=64] {'var'}, dimensions={0} | all-to-all | bytes 4194304 | tf_op jit(solution)/shard_map/all_to_all | solution.py:171
  420.8 0.0 copy-done
  420.8 10.7 %add_turned.1 = f32[16,3,64,256]{3,2,1,0:T(8,128)} custom-call(s32[32]{0:T(128)} %copy-done.2, f32[16,3,64,256]{3,2,1,0:T(8,128)} %copy-done, bf16[64,64,256]{2,1,0:T(8,128)(2,1)} %all_to_all.31.refs_0_.refs_1_, bf16[64,64,256]{2,1,0:T(8,128)(2,1)} %all_to_all.31.refs_0_.refs_1_), custom_call_target="tpu_custom_call" | custom-call | tf_op jit(solution)/shard_map/add_turned/pallas_call | solution.py:122
  (1 shorter events, 0.0 us)
Async XLA Ops:
  0.9 7.9 %copy-start.2 = (s32[32]{0:T(128)}, s32[32]{0:T(128)S(1)}, u32[]{:S(2)}) copy-start(s32[32]{0:T(128)S(1)} %reshape.25.index_ref) | copy-start | bytes 388
  1.0 7.8 %copy-start.3 = (s32[64]{0:T(128)}, s32[64]{0:T(128)S(1)}, u32[]{:S(2)}) copy-start(s32[64]{0:T(128)S(1)} %select_reduce_fusion.index_ref) | copy-start | bytes 772
  8.8 198.9 %all-to-all-start.1 = ((bf16[64,256,256]{2,1,0:T(8,128)(2,1)}), bf16[64,256,256]{2,1,0:T(8,128)(2,1)}, u32[]{:S(2)}, u32[]{:S(2)}) async-start(bf16[64,256,256]{2,1,0:T(8,128)(2,1)} %pick_columns.3), calls=%async_computation.1 | async-start | bytes 16777216 | tf_op jit(solution)/shard_map/all_to_all | solution.py:159
  207.7 30.8 %all-to-all-start = ((bf16[16,256,256]{2,1,0:T(8,128)(2,1)}), bf16[16,256,256]{2,1,0:T(8,128)(2,1)S(1)}, u32[]{:S(2)}, u32[]{:S(2)}) async-start(bf16[16,256,256]{2,1,0:T(8,128)(2,1)} %pick_columns.2), calls=%async_computation | async-start | bytes 4194304 | tf_op jit(solution)/shard_map/all_to_all | solution.py:155
  238.4 1.3 copy-start.1
  239.7 53.1 %all-to-all-start.2 = ((bf16[32,256,256]{2,1,0:T(8,128)(2,1)}), bf16[32,256,256]{2,1,0:T(8,128)(2,1)}, u32[]{:S(2)}, u32[]{:S(2)}) async-start(bf16[32,256,256]{2,1,0:T(8,128)(2,1)} %pick_blocks.2), calls=%async_computation.2 | async-start | bytes 8388608 | tf_op jit(solution)/shard_map/all_to_all | solution.py:162
  320.3 38.8 %all-to-all-start.3 = ((f32[16,3,64,256]{3,2,1,0:T(8,128)}), f32[16,3,64,256]{3,2,1,0:T(8,128)S(1)}, u32[]{:S(2)}, u32[]{:S(2)}) async-start(f32[16,3,64,256]{3,2,1,0:T(8,128)} %bitcast.9), calls=%async_computation.3 | async-start | bytes 6291456 | tf_op jit(solution)/shard_map/all_to_all | solution.py:169
  359.1 61.7 %copy-start = (f32[16,3,64,256]{3,2,1,0:T(8,128)}, f32[16,3,64,256]{3,2,1,0:T(8,128)S(1)}, u32[]{:S(2)}) copy-start(f32[16,3,64,256]{3,2,1,0:T(8,128)S(1)} %all-to-all-done.3.rows_ref) | copy-start | bytes 9437188
